TPU v7x, 32 devices: a whole 2x2x4 slice. The times are simulated.
32 devices in a mesh: site: 2 (over core), replica: 4 (over z), model: 4 (over y, x).
Axes of the slice: x: 2, y: 2, z: 4, core: 2. Of those that a mesh axis runs over, the one named last changes fastest.
Arguments:
- partial_query: bfloat16 [8, 1024, 1024], P(('site', 'replica'), None, 'model'), parts along dimension 0, may hold values from -4 to 4
- partial_key: bfloat16 [8, 1024, 1024], P(('site', 'replica'), None, 'model'), parts along dimension 0, may hold values from -4 to 4
- partial_value: bfloat16 [8, 1024, 1024], P(('site', 'replica'), None, 'model'), parts along dimension 0, may hold values from -4 to 4
- partial_mixed: bfloat16 [8, 1024, 1024], P(('site', 'replica'), 'model'), parts along dimension 0, may hold values from -4 to 4
- partial_norm: bfloat16 [8, 1024], P(('site', 'replica')), parts along dimension 0, may hold values from -8 to 8
- master_query: float32 [2048, 1024], P(('site', 'replica'), 'model'), parts along dimension 0, may hold values from -0.1875 to 0.1875
- master_key: float32 [2048, 1024], P(('site', 'replica'), 'model'), parts along dimension 0, may hold values from -0.1875 to 0.1875
- master_value: float32 [2048, 1024], P(('site', 'replica'), 'model'), parts along dimension 0, may hold values from -0.1875 to 0.1875
- master_mixed: float32 [2048, 1024], P(('site', 'model'), 'replica'), parts along dimension 0, may hold values from -0.1875 to 0.1875
- master_norm: float32 [2048], P(('site', 'replica')), parts along dimension 0, may hold values from 0.25 to 1.75
- memory_query: float32 [2048, 1024], P(('site', 'replica'), 'model'), parts along dimension 0, may hold values from 0.05 to 0.8
- memory_key: float32 [2048, 1024], P(('site', 'replica'), 'model'), parts along dimension 0, may hold values from 0.05 to 0.8
- memory_value: float32 [2048, 1024], P(('site', 'replica'), 'model'), parts along dimension 0, may hold values from 0.05 to 0.8
- memory_mixed: float32 [2048, 1024], P(('site', 'model'), 'replica'), parts along dimension 0, may hold values from 0.05 to 0.8
- memory_norm: float32 [2048], P(('site', 'replica')), parts along dimension 0, may hold values from 0.05 to 0.8
Outputs:
- compute_query: bfloat16 [2048, 1024], P('site', 'model'), parts along dimension 0
- compute_key: bfloat16 [2048, 1024], P('site', 'model'), parts along dimension 0
- compute_value: bfloat16 [2048, 1024], P('site', 'model'), parts along dimension 0
- compute_mixed: bfloat16 [2048, 1024], P(('site', 'model')), parts along dimension 0
- compute_norm: bfloat16 [2048], P('site'), parts along dimension 0
- stepped_query: float32 [2048, 1024], P(('site', 'replica'), 'model'), parts along dimension 0
- stepped_key: float32 [2048, 1024], P(('site', 'replica'), 'model'), parts along dimension 0
- stepped_value: float32 [2048, 1024], P(('site', 'replica'), 'model'), parts along dimension 0
- stepped_mixed: float32 [2048, 1024], P(('site', 'model'), 'replica'), parts along dimension 0
- stepped_norm: float32 [2048], P(('site', 'replica')), parts along dimension 0
- state_new_query: float32 [2048, 1024], P(('site', 'replica'), 'model'), parts along dimension 0
- state_new_key: float32 [2048, 1024], P(('site', 'replica'), 'model'), parts along dimension 0
- state_new_value: float32 [2048, 1024], P(('site', 'replica'), 'model'), parts along dimension 0
- state_new_mixed: float32 [2048, 1024], P(('site', 'model'), 'replica'), parts along dimension 0
- state_new_norm: float32 [2048], P(('site', 'replica')), parts along dimension 0
There are 2 independent parts, one for each index of `site`. A program takes and returns all parts, laid end to end along the dimension named above; each array names one. Nothing has to cross between parts.
All inputs are finite; a program needn't handle non-finite values.
Results may differ from a plain program's by a relative error of at most 0.001.
Values may be sent and summed in bfloat16 or wider, within the bound.
A program may use at most 64 MiB of HBM per device.

v0:
```python
import functools

import jax
import jax.numpy as jnp
from jax import lax
from jax.experimental import pallas as pl
from jax.experimental.pallas import tpu as pltpu
from jax.sharding import PartitionSpec as P

learn_rate = 0.05
hold_rate = 0.7
HALVES = 2
GAP = 1
LEAD = 2
MESH = pl.DeviceIdType.MESH
LINK = jnp.bfloat16
MATRICES = 4
LIMIT = 4.0
TOP = 120.0


def update(mean, master, memory):
    state = hold_rate * memory + (1.0 - hold_rate) * mean * mean
    return master - learn_rate * mean * lax.rsqrt(state + 1e-06), state


def encode(value, gain):
    size = jnp.exp2(jnp.abs(value) * gain - TOP)
    return jnp.where(value < 0, -size, size).astype(LINK)


def decode(code, step):
    code = code.astype(jnp.float32)
    size = (jnp.log2(jnp.abs(code)) + TOP) * step
    return jnp.where(code < 0, -size, size)


def kernel(n, halves, *refs):
    T = MATRICES
    (partial, master, memory) = refs[0:T], refs[T : 2 * T], refs[2 * T : 3 * T]
    norm_in = refs[3 * T]
    at = 3 * T + 1
    compute, stepped, state = refs[at : at + T], refs[at + T : at + 2 * T], refs[at + 2 * T : at + 3 * T]
    compute_norm, stepped_norm, state_norm = refs[at + 3 * T : at + 3 * T + 3]
    (
        tall, master_v, memory_v, send_v, recv_v, acc, step_v, state_v, tall_g, norm_v, load_sem,
        held_sem, rs_send, rs_recv, ag_send, ag_recv, norm_send, norm_recv, out_sem, gather_sem,
    ) = refs[at + 3 * T + 3 :]
    me = lax.axis_index("replica")
    rows, cols = master[0].shape
    part = rows // halves
    rate = n ** (-0.5)

    def spot(plane, c, s):
        top = pl.multiple_of(s * rows + (c % halves) * part, part)
        return plane.at[c // halves, pl.ds(top, part), :]

    def laid(plane, whole, t, out, sem):
        if t < T - 1:
            pairs = [(whole, plane.at[t])]
        else:
            pairs = [
                (whole.at[:, s * cols : (s + 1) * cols], plane.at[t, s * rows : (s + 1) * rows])
                for s in range(n)
            ]
        return [
            pltpu.make_async_copy(*(pair[::-1] if out else pair), sem.at[t, i])
            for i, pair in enumerate(pairs)
        ]

    loads = [laid(tall, partial[t], t, False, load_sem) for t in range(T)]
    held = [
        pltpu.make_async_copy(source[t], target.at[t], held_sem.at[i, t])
        for i, (source, target) in enumerate(((master, master_v), (memory, memory_v)))
        for t in range(T)
    ]
    for copy in sum(loads, []) + held:
        copy.start()

    barrier = pltpu.get_barrier_semaphore()
    for d in range(1, n):
        pl.semaphore_signal(
            barrier, inc=1, device_id={"replica": lax.rem(me + d, n)}, device_id_type=MESH
        )
    pl.semaphore_wait(barrier, n - 1)

    def norm_copy(d):
        return pltpu.make_async_remote_copy(
            src_ref=norm_in,
            dst_ref=norm_v.at[d - 1],
            send_sem=norm_send.at[d - 1],
            recv_sem=norm_recv.at[d - 1],
            device_id={"replica": lax.rem(me + d, n)},
            device_id_type=MESH,
        )

    def sum_copy(way, c, s, source=None):
        return pltpu.make_async_remote_copy(
            src_ref=send_v.at[way, c, s] if source is None else source,
            dst_ref=recv_v.at[way, c, s],
            send_sem=rs_send.at[way, c, s],
            recv_sem=rs_recv.at[way, c, s],
            device_id={"replica": me + 1 - 2 * way},
            device_id_type=MESH,
        )

    def share_copy(way, c, s):
        place = spot(tall_g, c, s)
        return pltpu.make_async_remote_copy(
            src_ref=place,
            dst_ref=place,
            send_sem=ag_send.at[way, c, s],
            recv_sem=ag_recv.at[way, c, s],
            device_id={"replica": me + 1 - 2 * way},
            device_id_type=MESH,
        )

    def terms(way):
        return me + 1 if way == 0 else n - me

    def gain(way):
        return (2 * TOP / LIMIT) / terms(way).astype(jnp.float32)

    def arrived(way, c, s):
        step = (terms(way) - 1).astype(jnp.float32) * (LIMIT / (2 * TOP))
        code = recv_v[way, c, s]
        return jnp.where(terms(way) == 2, code.astype(jnp.float32), decode(code, step))

    def behind(way):
        return me > 0 if way == 0 else me < n - 1

    def ahead(way, d):
        return me + d < n if way == 0 else me - d >= 0

    def either(way, d):
        return me + d if way == 0 else me - d

    def inner(c):
        return jnp.logical_and(c >= 0, c < count)

    def raw(c):
        for d in range(n - 1, 0, -1):
            for way in range(2):

                @pl.when(jnp.logical_and(ahead(way, d), jnp.logical_not(behind(way))))
                def _():
                    sum_copy(way, c, either(way, d), spot(tall, c, either(way, d))).start()

    def sums(way, c):
        for d in range(n - 1, 0, -1):
            s = either(way, d)

            @pl.when(jnp.logical_and(inner(c), jnp.logical_and(ahead(way, d), behind(way))))
            def _():
                own = spot(tall, c, s)[...].astype(jnp.float32)
                sum_copy(way, c, s).wait_recv()
                send_v[way, c, s] = encode(own + arrived(way, c, s), gain(way))
                sum_copy(way, c, s).start()

    def finish(c):
        acc[...] = spot(tall, c, me)[...].astype(jnp.float32)
        for way in range(2):

            @pl.when(behind(way))
            def _():
                sum_copy(way, c, me).wait_recv()
                acc[...] += arrived(way, c, me)

        t, band = c // halves, pl.ds(pl.multiple_of((c % halves) * part, part), part)
        new, held = update(acc[...] * rate, master_v[t, band, :], memory_v[t, band, :])
        spot(tall_g, c, me)[...] = new.astype(jnp.bfloat16)
        for way in range(2):

            @pl.when(ahead(way, 1))
            def _():
                share_copy(way, c, me).start()

        step_v[t, band, :] = new
        state_v[t, band, :] = held

    def forward(way, d, c, s):
        @pl.when(jnp.logical_and(inner(c), jnp.logical_and(s >= 0, s < n)))
        def _():
            share_copy(way, c, s).wait_recv()

            @pl.when(ahead(way, 1))
            def _():
                share_copy(way, c, s).start()

    def depth(s):
        return jnp.maximum(s, n - 1 - s)

    def step(at, carry):
        @pl.when(at + LEAD < count)
        def _():
            raw(at + LEAD)

        for way in range(2):
            sums(way, at - GAP * (terms(way) - 1))
        c = at - GAP * depth(me)

        @pl.when(inner(c))
        def _():
            finish(c)

        for d in range(1, n):
            for way in range(2):
                s = either(1 - way, d)
                forward(way, d, at - GAP * (depth(s) + d), s)
        return carry

    count = T * halves
    for t in range(T):
        for copy in loads[t]:
            copy.wait()
        for c in range(t * halves, (t + 1) * halves):
            if c < LEAD:
                raw(c)
    for d in range(1, n):
        norm_copy(d).start()
    for copy in held:
        copy.wait()

    outs = [
        pltpu.make_async_copy(source.at[t], target[t], out_sem.at[i, t])
        for t in range(T)
        for i, (source, target) in enumerate(((step_v, stepped), (state_v, state)))
    ]
    gathered = [laid(tall_g, compute[t], t, True, gather_sem) for t in range(T)]
    tasks = sorted(
        [(t * halves + halves - 1 + GAP * (n - 1), outs[2 * t : 2 * t + 2]) for t in range(T)]
        + [(t * halves + halves - 1 + 2 * GAP * (n - 1), gathered[t]) for t in range(T)],
        key=lambda task: task[0],
    )
    reached = 0
    for last, copies in tasks:
        if last >= reached:
            lax.fori_loop(reached, last + 1, step, 0)
            reached = last + 1
        for copy in copies:
            copy.start()

    whole = norm_in.shape[1] - 2 * cols
    for d in range(1, n):
        norm_copy(d).wait()
    mean_norm = norm_in[:, :whole]
    for d in range(1, n):
        mean_norm = mean_norm + norm_v[d - 1][:, :whole]
    mean_norm = mean_norm * rate
    for s in range(n):
        mean_s = mean_norm[:, s * cols : (s + 1) * cols]

        @pl.when(me == s)
        def _():
            new, held = update(mean_s, norm_in[:, whole : whole + cols], norm_in[:, whole + cols :])
            stepped_norm[...] = new
            state_norm[...] = held
            compute_norm[:, s * cols : (s + 1) * cols] = new.astype(jnp.bfloat16)

        @pl.when(me != s)
        def _():
            slot = lax.rem(me - s + n, n) - 1
            new, held = update(
                mean_s, norm_v[slot, :, whole : whole + cols], norm_v[slot, :, whole + cols :]
            )
            compute_norm[:, s * cols : (s + 1) * cols] = new.astype(jnp.bfloat16)

    def drain(c, carry):
        for way in range(2):
            for d in range(1, n):

                @pl.when(ahead(way, d))
                def _():
                    sum_copy(way, c, either(way, d)).wait_send()

            for d in range(n):
                s = either(1 - way, d)

                @pl.when(jnp.logical_and(jnp.logical_and(s >= 0, s < n), ahead(way, 1)))
                def _():
                    share_copy(way, c, s).wait_send()

        return carry

    lax.fori_loop(0, count, drain, 0)
    for copy in outs + sum(gathered, []):
        copy.wait()


def line(n, partials, masters, memories, partial_norm, master_norm, memory_norm):
    T, halves = MATRICES, HALVES
    rows, cols = masters[0].shape
    part = rows // halves
    count = T * halves
    whole = partial_norm.shape[1]
    norm_in = jnp.concatenate(
        [partial_norm.astype(jnp.float32), master_norm[None], memory_norm[None]], axis=1
    )
    f32, bf16 = jnp.float32, jnp.bfloat16
    anywhere = pl.BlockSpec(memory_space=pl.ANY)
    inside = pl.BlockSpec(memory_space=pltpu.VMEM)
    share = jax.ShapeDtypeStruct((rows, cols), f32)
    dma = pltpu.SemaphoreType.DMA
    out = pl.pallas_call(
        functools.partial(kernel, n, halves),
        out_shape=[jax.ShapeDtypeStruct(p.shape, bf16) for p in partials]
        + [share] * (2 * T)
        + [jax.ShapeDtypeStruct((1, whole), bf16)]
        + [jax.ShapeDtypeStruct((1, cols), f32)] * 2,
        in_specs=[anywhere] * (3 * T) + [inside],
        out_specs=[anywhere] * (3 * T) + [inside] * 3,
        scratch_shapes=[
            pltpu.VMEM((T, n * rows, cols), bf16),
            pltpu.VMEM((T, rows, cols), f32),
            pltpu.VMEM((T, rows, cols), f32),
            pltpu.VMEM((2, count, n, part, cols), LINK),
            pltpu.VMEM((2, count, n, part, cols), LINK),
            pltpu.VMEM((part, cols), f32),
            pltpu.VMEM((T, rows, cols), f32),
            pltpu.VMEM((T, rows, cols), f32),
            pltpu.VMEM((T, n * rows, cols), bf16),
            pltpu.VMEM((n - 1, 1, whole + 2 * cols), f32),
            dma((T, n)),
            dma((2, T)),
            dma((2, count, n)),
            dma((2, count, n)),
            dma((2, count, n)),
            dma((2, count, n)),
            dma((n - 1,)),
            dma((n - 1,)),
            dma((2, T)),
            dma((T, n)),
        ],
        compiler_params=pltpu.CompilerParams(collective_id=0, has_side_effects=True),
        name="line_step",
    )(*partials, *masters, *memories, norm_in)
    compute, stepped, state = out[:T], out[T : 2 * T], out[2 * T : 3 * T]
    compute_norm, stepped_norm, state_norm = out[3 * T :]
    return (*compute, compute_norm[0], *stepped, stepped_norm[0], *state, state_norm[0])


def plain(n, partials, masters, memories, partial_norm, master_norm, memory_norm):
    rate = n ** (-0.5)
    axes = (0, 0, 0, 1)
    compute, stepped, state = [], [], []
    for p, master, memory, axis in zip(partials, masters, memories, axes):
        total = lax.psum_scatter(
            p.astype(jnp.float32), "replica", scatter_dimension=axis, tiled=True
        )
        new, held = update(total * rate, master, memory)
        stepped.append(new)
        state.append(held)
    whole = lax.psum(partial_norm[0].astype(jnp.float32), "replica")
    size = master_norm.shape[0]
    mean = lax.dynamic_slice_in_dim(whole, lax.axis_index("replica") * size, size) * rate
    new, held = update(mean, master_norm, memory_norm)
    stepped.append(new)
    state.append(held)
    for new, axis in zip(stepped, axes + (0,)):
        compute.append(lax.all_gather(new.astype(jnp.bfloat16), "replica", axis=axis, tiled=True))
    return (*compute, *stepped, *state)


def body(*args):
    partials = [p[0] for p in args[:4]]
    partial_norm = args[4]
    masters, master_norm = args[5:9], args[9]
    memories, memory_norm = args[10:14], args[14]
    n = lax.axis_size("replica")
    shapes = {m.shape for m in masters}
    rows, cols = masters[0].shape
    fits = (
        1 < n <= 4
        and len(shapes) == 1
        and rows % (32 * HALVES) == 0
        and cols % 128 == 0
        and master_norm.shape[0] == cols
    )
    form = line if fits else plain
    return form(n, partials, masters, memories, partial_norm, master_norm, memory_norm)


def solution(mesh):
    tall = P(("site", "replica"), None, "model")
    share, flat = P(("site", "replica"), "model"), P(("site", "replica"))
    wide = P(("site", "model"), "replica")
    shares = (share, share, share, wide, flat)
    return jax.shard_map(
        body,
        mesh=mesh,
        in_specs=(
            tall,
            tall,
            tall,
            P(("site", "replica"), "model", None),
            P(("site", "replica"), None),
            *shares,
            *shares,
        ),
        out_specs=(
            P("site", "model"),
            P("site", "model"),
            P("site", "model"),
            P(("site", "model"), None),
            P("site"),
            *shares,
            *shares,
        ),
        check_vma=False,
    )
```

profile of v0, /device:TPU:0, one launch (start us, length us, event | category | flops | bytes accessed | tf_op | source)
XLA Modules:
  0.0 94.7 jit_solution(12200250818720680237)
XLA Ops:
  0.6 0.0 copy-start.11
  0.7 0.7 copy-done.11
  1.3 0.0 copy-start.13
  1.3 0.0 copy-start.14
  1.3 0.7 copy-done.13
  2.0 0.0 copy-done.14
  2.0 0.6 pad_maximum_fusion.refs_12_
  2.6 76.5 %line_step.1 = (bf16[1024,256]{1,0:T(8,128)(2,1)}, bf16[1024,256]{1,0:T(8,128)(2,1)}, bf16[1024,256]{1,0:T(8,128)(2,1)}, bf16[256,1024]{1,0:T(8,128)(2,1)}, f32[...) custom-call(bf16[1024,256]{1,0:T(8,128)(2,1)} %bitcast.8, ...), custom_call_target="tpu_custom_call" | custom-call | tf_op jit(solution)/shard_map/line_step/pallas_call | solution.py:304
  79.1 0.0 copy-start.12
  79.1 0.7 copy-done.12
  79.8 0.6 reduce
  80.4 0.0 copy-start.2
  80.4 1.9 %copy.44 = bf16[1024,256]{1,0:T(8,128)(2,1)} copy(bf16[1024,256]{1,0:T(8,128)(2,1)} %get-tuple-element.60) | data formatting | bytes 1048576
  82.3 0.0 copy-done.2
  82.3 0.0 copy-start.1
  82.3 0.8 copy.45
  83.1 0.4 copy-done.1
  83.6 0.0 copy-start
  83.6 0.8 copy.46
  84.4 0.4 copy-done
  84.8 0.0 copy-start.10
  84.8 0.8 copy.47
  85.6 0.3 copy-done.10
  85.9 0.0 copy-start.9
  85.9 0.7 copy.48
  86.6 0.3 copy-done.9
  86.9 0.0 copy-start.8
  86.9 0.7 copy.49
  87.6 0.3 copy-done.8
  88.0 0.0 copy-start.7
  88.0 0.7 copy.50
  88.7 0.3 copy-done.7
  89.0 0.0 copy-start.16
  89.0 0.0 copy-start.6
  89.0 0.7 copy.51
  89.7 0.0 copy-done.16
  89.7 0.6 copy.52
  90.3 0.0 copy-done.6
  90.3 0.0 copy-start.5
  90.3 0.7 copy.53
  91.0 0.3 copy-done.5
  91.3 0.0 copy-start.4
  91.3 0.7 copy.54
  92.0 0.3 copy-done.4
  92.4 0.0 copy-start.3
  92.4 0.7 copy.55
  93.1 0.3 copy-done.3
  93.4 0.0 copy-start.15
  93.4 0.7 copy.56
  94.1 0.0 copy-done.15
  94.1 0.6 copy.57
  (1 shorter events, 0.0 us)
Async XLA Ops:
  0.6 0.7 copy-start.11
  1.3 0.7 copy-start.13
  1.3 0.7 copy-start.14
  79.1 0.7 copy-start.12
  80.4 1.9 %copy-start.2 = (bf16[1024,256]{1,0:T(8,128)(2,1)S(1)}, bf16[1024,256]{1,0:T(8,128)(2,1)}, u32[]{:S(2)}) copy-start(bf16[1024,256]{1,0:T(8,128)(2,1)} %get-tuple-element.61) | copy-start | bytes 1572868
  82.3 1.2 %copy-start.1 = (bf16[1024,256]{1,0:T(8,128)(2,1)S(1)}, bf16[1024,256]{1,0:T(8,128)(2,1)}, u32[]{:S(2)}) copy-start(bf16[1024,256]{1,0:T(8,128)(2,1)} %get-tuple-element.62) | copy-start | bytes 1572868
  83.6 1.2 %copy-start = (bf16[256,1024]{1,0:T(8,128)(2,1)S(1)}, bf16[256,1024]{1,0:T(8,128)(2,1)}, u32[]{:S(2)}) copy-start(bf16[256,1024]{1,0:T(8,128)(2,1)} %get-tuple-element.63) | copy-start | bytes 1572868
  84.8 1.1 %copy-start.10 = (f32[256,256]{1,0:T(8,128)S(1)}, f32[256,256]{1,0:T(8,128)}, u32[]{:S(2)}) copy-start(f32[256,256]{1,0:T(8,128)} %get-tuple-element.65) | copy-start | bytes 786436
  85.9 1.0 %copy-start.9 = (f32[256,256]{1,0:T(8,128)S(1)}, f32[256,256]{1,0:T(8,128)}, u32[]{:S(2)}) copy-start(f32[256,256]{1,0:T(8,128)} %get-tuple-element.66) | copy-start | bytes 786436
  86.9 1.0 %copy-start.8 = (f32[256,256]{1,0:T(8,128)S(1)}, f32[256,256]{1,0:T(8,128)}, u32[]{:S(2)}) copy-start(f32[256,256]{1,0:T(8,128)} %get-tuple-element.67) | copy-start | bytes 786436
  88.0 1.0 %copy-start.7 = (f32[256,256]{1,0:T(8,128)S(1)}, f32[256,256]{1,0:T(8,128)}, u32[]{:S(2)}) copy-start(f32[256,256]{1,0:T(8,128)} %get-tuple-element.68) | copy-start | bytes 786436
  89.0 0.7 copy-start.16
  89.0 1.3 %copy-start.6 = (f32[256,256]{1,0:T(8,128)S(1)}, f32[256,256]{1,0:T(8,128)}, u32[]{:S(2)}) copy-start(f32[256,256]{1,0:T(8,128)} %get-tuple-element.70) | copy-start | bytes 786436
  90.3 1.0 %copy-start.5 = (f32[256,256]{1,0:T(8,128)S(1)}, f32[256,256]{1,0:T(8,128)}, u32[]{:S(2)}) copy-start(f32[256,256]{1,0:T(8,128)} %get-tuple-element.71) | copy-start | bytes 786436
  91.3 1.0 %copy-start.4 = (f32[256,256]{1,0:T(8,128)S(1)}, f32[256,256]{1,0:T(8,128)}, u32[]{:S(2)}) copy-start(f32[256,256]{1,0:T(8,128)} %get-tuple-element.72) | copy-start | bytes 786436
  92.4 1.0 %copy-start.3 = (f32[256,256]{1,0:T(8,128)S(1)}, f32[256,256]{1,0:T(8,128)}, u32[]{:S(2)}) copy-start(f32[256,256]{1,0:T(8,128)} %get-tuple-element.73) | copy-start | bytes 786436
  93.4 0.7 copy-start.15
where the time goes:
time: 95.3 us; the launch traced here: 94.7 us
  Pallas kernels  76.5 us (80%)
  local copies, waits for them, and re-layouts  16.3 us (17%)
  other arithmetic  1.2 us (1%)
    pallas_call x1, Pallas kernels, line(): pl.pallas_call(functools.partial(kernel, n, halves), out_shape=[jax.Shape...  76.5 us
    unnamed x48, local copies, waits for them, and re-layouts  16.3 us

commit v1 on v0

v1 whole, which is shorter than its diff:
```python
import functools

import jax
import jax.numpy as jnp
from jax import lax
from jax.experimental import pallas as pl
from jax.experimental.pallas import tpu as pltpu
from jax.sharding import PartitionSpec as P

learn_rate = 0.05
hold_rate = 0.7
HALVES = 4
DEPTH = 2
END_CLOSE = 8
RS_OUT = 0
RS_BACK = 1
FINISH = 2
PASS_OUT = 10
PASS_NEAR = 4
PASS_FAR = 14
MESH = pl.DeviceIdType.MESH
LINK = jnp.bfloat16
MATRICES = 4
LIMIT = 4.0
TOP = 125.0


def update(mean, master, memory):
    state = hold_rate * memory + (1.0 - hold_rate) * mean * mean
    return master - learn_rate * mean * lax.rsqrt(state + 1e-06), state


def encode(value, terms):
    gain = TOP / (terms * LIMIT)
    return jnp.exp2(value * gain).astype(LINK)


def decode(code, terms):
    return jnp.log2(code.astype(jnp.float32)) * (terms * LIMIT / TOP)


def kernel(n, halves, *refs):
    T = MATRICES
    (partial, master, memory) = refs[0:T], refs[T : 2 * T], refs[2 * T : 3 * T]
    norms_in = refs[3 * T : 3 * T + 3]
    at = 3 * T + 3
    grown, step_v, state_v, compute_norm, stepped_norm, state_norm = refs[at : at + 6]
    (
        tall, master_v, memory_v, send_v, recv_v, norm_p, norm_m, norm_k,
        load_sem, held_sem, norm_load, rs_recv, ag_recv, end_recv, sent, raw_sent, norm_send, norm_recv,
    ) = refs[at + 6 :]
    norms_v = (norm_p, norm_m, norm_k)
    me = lax.axis_index("replica")
    rows, cols = master[0].shape
    part = rows // halves
    count = T * halves
    rate = n ** (-0.5)
    flip = jnp.where(me >= n // 2, 1, 0)
    out, back = flip, 1 - flip
    is_end = jnp.logical_or(me == 0, me == n - 1)

    def seg(s):
        return flip * (n - 1) + (1 - 2 * flip) * s

    def peer(way):
        return {"replica": me + 1 - 2 * way}

    def spot(plane, c, s):
        top = pl.multiple_of(s * rows + lax.rem(c, halves) * part, part)
        return plane.at[lax.div(c, halves), pl.ds(top, part), :]

    def loads_of(t):
        if t < T - 1:
            pairs = [(partial[t], tall.at[t])]
        else:
            pairs = [
                (partial[t].at[:, s * cols : (s + 1) * cols], tall.at[t, s * rows : (s + 1) * rows])
                for s in range(n)
            ]
        return [pltpu.make_async_copy(*pair, load_sem.at[t, i]) for i, pair in enumerate(pairs)]

    loads = [loads_of(t) for t in range(T)]
    own_norms = [
        pltpu.make_async_copy(source, target.at[me], norm_load.at[i])
        for i, (source, target) in enumerate(zip(norms_in, norms_v))
    ]
    held = [
        pltpu.make_async_copy(source[t], target.at[t], held_sem.at[i, t])
        for i, (source, target) in enumerate(((master, master_v), (memory, memory_v)))
        for t in range(T)
    ]
    for copy in sum(loads, []) + own_norms + held:
        copy.start()

    barrier = pltpu.get_barrier_semaphore()

    @pl.when(me > 0)
    def _():
        pl.semaphore_signal(barrier, inc=1, device_id=peer(1), device_id_type=MESH)

    @pl.when(me < n - 1)
    def _():
        pl.semaphore_signal(barrier, inc=1, device_id=peer(0), device_id_type=MESH)

    pl.semaphore_wait(barrier, jnp.where(is_end, 1, 2))

    def sum_copy(way, c, s, source):
        return pltpu.make_async_remote_copy(
            src_ref=source,
            dst_ref=recv_v.at[way, c, s],
            send_sem=sent.at[way],
            recv_sem=rs_recv.at[way, c, s],
            device_id=peer(way),
            device_id_type=MESH,
        )

    def sum_wait(way, c, s):
        sum_copy(way, c, s, send_v.at[0, c]).wait_recv()

    def share_copy(way, c, s, last=False):
        place = spot(grown, c, s)
        return pltpu.make_async_remote_copy(
            src_ref=place,
            dst_ref=place,
            send_sem=sent.at[way],
            recv_sem=end_recv.at[0] if last else ag_recv.at[way, c, s],
            device_id=peer(way),
            device_id_type=MESH,
        )

    def norm_copies(way, s):
        return [
            pltpu.make_async_remote_copy(
                src_ref=ref.at[s],
                dst_ref=ref.at[s],
                send_sem=norm_send.at[way, s, i],
                recv_sem=norm_recv.at[s, i],
                device_id=peer(way),
                device_id_type=MESH,
            )
            for i, ref in enumerate(norms_v)
        ]

    def finish(c, total, s):
        t = lax.div(c, halves)
        band = pl.ds(pl.multiple_of(lax.rem(c, halves) * part, part), part)
        new, held_new = update(total * rate, master_v[t, band, :], memory_v[t, band, :])
        spot(grown, c, s)[...] = new.astype(jnp.bfloat16)
        step_v[t, band, :] = new
        state_v[t, band, :] = held_new

    def own(c, s):
        return spot(tall, c, s)[...].astype(jnp.float32)

    def sent_wait(way, planes):
        pltpu.make_async_remote_copy(
            src_ref=tall.at[0:planes],
            dst_ref=grown.at[0:planes],
            send_sem=sent.at[way],
            recv_sem=end_recv.at[0],
            device_id=peer(way),
            device_id_type=MESH,
        ).wait_send()

    @pl.when(is_end)
    def _():
        for copy in own_norms:
            copy.wait()
        for copy in norm_copies(out, me):
            copy.start()

        def raw_copy(c, s):
            return pltpu.make_async_remote_copy(
                src_ref=spot(tall, c, s),
                dst_ref=recv_v.at[out, c, s],
                send_sem=raw_sent.at[lax.rem(c, DEPTH), s],
                recv_sem=rs_recv.at[out, c, s],
                device_id=peer(out),
                device_id_type=MESH,
            )

        def close(c):
            sum_wait(back, c, me)
            finish(c, own(c, me) + decode(recv_v[back, c, me], n - 1), me)
            share_copy(out, c, me).start()

        def end_step(j, carry):
            for s in range(n - 1, 0, -1):

                @pl.when(jnp.logical_and(j >= DEPTH, j < count + DEPTH))
                def _():
                    raw_copy(j - DEPTH, seg(s)).wait_send()

                @pl.when(j < count)
                def _():
                    raw_copy(j, seg(s)).start()

            @pl.when(jnp.logical_and(j >= END_CLOSE, j < count + END_CLOSE))
            def _():
                close(j - END_CLOSE)

            return carry

        for t in range(T):
            for copy in loads[t]:
                copy.wait()
            if t == 1:
                for copy in held:
                    copy.wait()
            lax.fori_loop(t * halves, (t + 1) * halves, end_step, 0)
        lax.fori_loop(count, count + max(DEPTH, END_CLOSE), end_step, 0)
        for copy in norm_copies(out, me):
            copy.wait_send()
        for s in range(1, n):
            for copy in norm_copies(out, seg(s)):
                copy.wait_recv()

    @pl.when(jnp.logical_not(is_end))
    def _():
        for copy in own_norms:
            copy.wait()
        for way in range(2):
            for copy in norm_copies(way, me):
                copy.start()
        for copy in sum(loads, []) + held:
            copy.wait()

        def step(j, carry):
            def at_lag(lag, act):
                c = j - lag

                @pl.when(jnp.logical_and(c >= 0, c < count))
                def _():
                    act(c)

            def rs_out(c):
                for i, s in enumerate((seg(3), seg(2))):
                    sum_wait(out, c, s)
                    total = own(c, s) + recv_v[out, c, s].astype(jnp.float32)
                    send_v[i, c] = encode(total, 2)
                    sum_copy(out, c, s, send_v.at[i, c]).start()

            def rs_back(c):
                s = seg(0)
                sum_wait(back, c, s)
                send_v[2, c] = encode(own(c, s) + decode(recv_v[back, c, s], 2), 3)
                sum_copy(back, c, s, send_v.at[2, c]).start()

            def close(c):
                sum_wait(out, c, me)
                total = own(c, me) + recv_v[out, c, me].astype(jnp.float32)
                sum_wait(back, c, me)
                finish(c, total + decode(recv_v[back, c, me], 2), me)
                share_copy(out, c, me).start()
                share_copy(back, c, me, True).start()

            def pass_on(way, s, last):
                def act(c):
                    share_copy(way, c, s).wait_recv()
                    share_copy(way, c, s, last).start()

                return act

            at_lag(RS_OUT, rs_out)
            at_lag(RS_BACK, rs_back)
            at_lag(FINISH, close)
            at_lag(PASS_OUT, pass_on(out, seg(0), False))
            at_lag(PASS_NEAR, pass_on(back, seg(2), True))
            at_lag(PASS_FAR, pass_on(back, seg(3), True))
            return carry

        early = 2
        lax.fori_loop(0, early, step, 0)
        for way, s in ((out, 0), (back, 2)):
            for copy in norm_copies(way, seg(s)):
                copy.wait_recv()
            for copy in norm_copies(way, seg(s)):
                copy.start()
        lax.fori_loop(early, 2 * early, step, 0)
        for copy in norm_copies(back, seg(3)):
            copy.wait_recv()
        for copy in norm_copies(back, seg(3)):
            copy.start()
        last = max(RS_OUT, RS_BACK, FINISH, PASS_OUT, PASS_NEAR, PASS_FAR)
        lax.fori_loop(2 * early, count + last, step, 0)
        for way, s in ((out, 0), (out, 1), (back, 1), (back, 2), (back, 3)):
            for copy in norm_copies(way, seg(s)):
                copy.wait_send()

    mean = norm_p[0].astype(jnp.float32)
    for s in range(1, n):
        mean = mean + norm_p[s].astype(jnp.float32)
    mean = mean * rate
    for s in range(n):
        new, held_new = update(mean[:, s * cols : (s + 1) * cols], norm_m[s], norm_k[s])
        compute_norm[:, s * cols : (s + 1) * cols] = new

        @pl.when(me == s)
        def _():
            stepped_norm[...] = new
            state_norm[...] = held_new

    @pl.when(jnp.logical_not(is_end))
    def _():
        sent_wait(out, T)
        sent_wait(back, T)

    @pl.when(is_end)
    def _():
        sent_wait(out, 1)
        three = grown.at[0 : n - 1]
        pltpu.make_async_remote_copy(
            src_ref=three,
            dst_ref=three,
            send_sem=sent.at[out],
            recv_sem=end_recv.at[0],
            device_id=peer(out),
            device_id_type=MESH,
        ).wait_recv()


def write(n, *refs):
    T = MATRICES
    grown, step_v, state_v, stepped_norm_v, state_norm_v = refs[:5]
    compute, stepped, state = refs[5 : 5 + T], refs[5 + T : 5 + 2 * T], refs[5 + 2 * T : 5 + 3 * T]
    stepped_norm, state_norm, sems = refs[5 + 3 * T :]
    rows, cols = stepped[0].shape
    pairs = [(grown.at[t], compute[t]) for t in range(T - 1)]
    pairs += [
        (grown.at[T - 1, s * rows : (s + 1) * rows], compute[T - 1].at[:, s * cols : (s + 1) * cols])
        for s in range(n)
    ]
    pairs += [(step_v.at[t], stepped[t]) for t in range(T)]
    pairs += [(state_v.at[t], state[t]) for t in range(T)]
    pairs += [(stepped_norm_v, stepped_norm), (state_norm_v, state_norm)]
    copies = [pltpu.make_async_copy(*pair, sems.at[i]) for i, pair in enumerate(pairs)]
    for copy in copies:
        copy.start()
    for copy in copies:
        copy.wait()


def line(n, partials, masters, memories, partial_norm, master_norm, memory_norm):
    T, halves = MATRICES, HALVES
    rows, cols = masters[0].shape
    part = rows // halves
    count = T * halves
    whole = partial_norm.shape[1]
    f32, bf16 = jnp.float32, jnp.bfloat16
    anywhere = pl.BlockSpec(memory_space=pl.ANY)
    inside = pl.BlockSpec(memory_space=pltpu.VMEM)
    dma = pltpu.SemaphoreType.DMA
    kept = pl.pallas_call(
        functools.partial(kernel, n, halves),
        out_shape=[
            pltpu.VMEM((T, n * rows, cols), bf16),
            pltpu.VMEM((T, rows, cols), f32),
            pltpu.VMEM((T, rows, cols), f32),
            pltpu.VMEM((1, whole), f32),
            pltpu.VMEM((1, cols), f32),
            pltpu.VMEM((1, cols), f32),
        ],
        in_specs=[anywhere] * (3 * T + 3),
        out_specs=[inside] * 6,
        scratch_shapes=[
            pltpu.VMEM((T, n * rows, cols), bf16),
            pltpu.VMEM((T, rows, cols), f32),
            pltpu.VMEM((T, rows, cols), f32),
            pltpu.VMEM((n - 1, count, part, cols), LINK),
            pltpu.VMEM((2, count, n, part, cols), LINK),
            pltpu.VMEM((n, 1, whole), bf16),
            pltpu.VMEM((n, 1, cols), f32),
            pltpu.VMEM((n, 1, cols), f32),
            dma((T, n)),
            dma((2, T)),
            dma((3,)),
            dma((2, count, n)),
            dma((2, count, n)),
            dma((1,)),
            dma((2,)),
            dma((DEPTH, n)),
            dma((2, n, 3)),
            dma((n, 3)),
        ],
        compiler_params=pltpu.CompilerParams(
            collective_id=0, has_side_effects=True, vmem_limit_bytes=32 * 1024 * 1024
        ),
        name="line_step",
    )(
        *(
            pltpu.with_memory_space_constraint(x, pltpu.HBM)
            for x in (
                *partials, *masters, *memories, partial_norm, master_norm[None], memory_norm[None],
            )
        )
    )
    share = jax.ShapeDtypeStruct((rows, cols), f32)
    out = pl.pallas_call(
        functools.partial(write, n),
        out_shape=[jax.ShapeDtypeStruct(p.shape, bf16) for p in partials]
        + [share] * (2 * T)
        + [jax.ShapeDtypeStruct((1, cols), f32)] * 2,
        in_specs=[inside] * 5,
        out_specs=[anywhere] * (3 * T + 2),
        scratch_shapes=[dma((3 * T + n + 1,))],
        compiler_params=pltpu.CompilerParams(vmem_limit_bytes=1024 * 1024),
        name="write_out",
    )(*kept[:3], *kept[4:])
    compute, stepped, state = out[:T], out[T : 2 * T], out[2 * T : 3 * T]
    stepped_norm, state_norm = out[3 * T :]
    compute_norm = kept[3][0].astype(bf16)
    return (*compute, compute_norm, *stepped, stepped_norm[0], *state, state_norm[0])


def plain(n, partials, masters, memories, partial_norm, master_norm, memory_norm):
    rate = n ** (-0.5)
    axes = (0, 0, 0, 1)
    compute, stepped, state = [], [], []
    for p, master, memory, axis in zip(partials, masters, memories, axes):
        total = lax.psum_scatter(
            p.astype(jnp.float32), "replica", scatter_dimension=axis, tiled=True
        )
        new, held = update(total * rate, master, memory)
        stepped.append(new)
        state.append(held)
    whole = lax.psum(partial_norm[0].astype(jnp.float32), "replica")
    size = master_norm.shape[0]
    mean = lax.dynamic_slice_in_dim(whole, lax.axis_index("replica") * size, size) * rate
    new, held = update(mean, master_norm, memory_norm)
    stepped.append(new)
    state.append(held)
    for new, axis in zip(stepped, axes + (0,)):
        compute.append(lax.all_gather(new.astype(jnp.bfloat16), "replica", axis=axis, tiled=True))
    return (*compute, *stepped, *state)


def body(*args):
    partials = [p[0] for p in args[:4]]
    partial_norm = args[4]
    masters, master_norm = args[5:9], args[9]
    memories, memory_norm = args[10:14], args[14]
    n = lax.axis_size("replica")
    shapes = {m.shape for m in masters}
    rows, cols = masters[0].shape
    fits = (
        n == MATRICES
        and len(shapes) == 1
        and rows % (32 * HALVES) == 0
        and cols % 128 == 0
        and master_norm.shape[0] == cols
    )
    form = line if fits else plain
    return form(n, partials, masters, memories, partial_norm, master_norm, memory_norm)


def solution(mesh):
    tall = P(("site", "replica"), None, "model")
    share, flat = P(("site", "replica"), "model"), P(("site", "replica"))
    wide = P(("site", "model"), "replica")
    shares = (share, share, share, wide, flat)
    return jax.shard_map(
        body,
        mesh=mesh,
        in_specs=(
            tall,
            tall,
            tall,
            P(("site", "replica"), "model", None),
            P(("site", "replica"), None),
            *shares,
            *shares,
        ),
        out_specs=(
            P("site", "model"),
            P("site", "model"),
            P("site", "model"),
            P(("site", "model"), None),
            P("site"),
            *shares,
            *shares,
        ),
        check_vma=False,
    )
```

time: 95.3 us -> 70.4 us (0.74)
  local copies, waits for them, and re-layouts: 16.3 us -> 0 us
  Pallas kernels: 76.5 us -> 69 us
    unnamed x48 -> x0, local copies, waits for them, and re-layouts: 16.3 us -> none
    pallas_call x1 -> x2, Pallas kernels: 76.5 us -> 69 us  [the longest x1 66.9 us: line(): pl.pallas_call(functools.partial(kernel, n, halves), out_shape=[pltpu.VME...]
where the time goes in v1:
time: 70.4 us; the launch traced here: 70.3 us
  Pallas kernels  69 us (98%)
    pallas_call x1, Pallas kernels, line(): pl.pallas_call(functools.partial(kernel, n, halves), out_shape=[pltpu.VME...  66.9 us
    pallas_call x1, Pallas kernels, line(): pl.pallas_call(functools.partial(write, n), out_shape=[jax.ShapeDtypeStru...  2.16 us

profile of v1, /device:TPU:0, one launch (start us, length us, event | category | flops | bytes accessed | tf_op | source)
XLA Modules:
  0.0 70.3 jit_solution(17313473410232747005)
XLA Ops:
  0.7 66.9 %line_step.1 = (bf16[4,1024,256]{2,1,0:T(8,128)(2,1)S(1)}, f32[4,256,256]{2,1,0:T(8,128)S(1)}, f32[4,256,256]{2,1,0:T(8,128)S(1)}, f32[1,1024]{1,0:T(1,128)S(1)}...) custom-call(bf16[1024,256]{1,0:T(8,128)(2,1)} %bitcast.8, bf16[1024,256]{1,0:T(8,128)(2,1)} %bitcast.9, ...), custom_call_target="tpu_custom_call" | custom-call | tf_op jit(solution)/shard_map/line_step/pallas_call | solution.py:353
  67.5 2.2 %write_out.1 = (bf16[1024,256]{1,0:T(8,128)(2,1)}, bf16[1024,256]{1,0:T(8,128)(2,1)}, bf16[1024,256]{1,0:T(8,128)(2,1)}, bf16[256,1024]{1,0:T(8,128)(2,1)}, f32[...) custom-call(bf16[4,1024,256]{2,1,0:T(8,128)(2,1)S(1)} %get-tuple-ele, ...), custom_call_target="tpu_custom_call" | custom-call | tf_op jit(solution)/shard_map/write_out/pallas_call | solution.py:398
  69.7 0.6 convert_reduce_fusion

commit v2 on v1

--- a/solution.py
+++ b/solution.py
@@ -11,13 +11,9 @@
 hold_rate = 0.7
 HALVES = 4
 DEPTH = 2
-END_CLOSE = 8
-RS_OUT = 0
-RS_BACK = 1
-FINISH = 2
-PASS_OUT = 10
-PASS_NEAR = 4
-PASS_FAR = 14
+EARLY = 3
+ENDS = (("raw3", 0), ("close", 47), ("raw1", 3), ("raw2", 0))
+MIDDLES = (("pass2", 7), ("close", 4), ("pass3", 26), ("pass0", 18), ("sum3", 0), ("sum0", 2), ("sum2", 1))
 MESH = pl.DeviceIdType.MESH
 LINK = jnp.bfloat16
 MATRICES = 4
@@ -89,9 +85,8 @@
         for i, (source, target) in enumerate(((master, master_v), (memory, memory_v)))
         for t in range(T)
     ]
-    for copy in sum(loads, []) + own_norms + held:
+    for copy in loads[0]:
         copy.start()
-
     barrier = pltpu.get_barrier_semaphore()
 
     @pl.when(me > 0)
@@ -102,6 +97,8 @@
     def _():
         pl.semaphore_signal(barrier, inc=1, device_id=peer(0), device_id_type=MESH)
 
+    for copy in sum(loads[1:], []) + own_norms + held:
+        copy.start()
     pl.semaphore_wait(barrier, jnp.where(is_end, 1, 2))
 
     def sum_copy(way, c, s, source):
@@ -152,6 +149,21 @@
     def own(c, s):
         return spot(tall, c, s)[...].astype(jnp.float32)
 
+    def run(table, acts, low=None, high=None):
+        def step(j, carry):
+            for name, lag in table:
+                c = j - lag
+
+                @pl.when(jnp.logical_and(c >= 0, c < count))
+                def _():
+                    acts[name](c)
+
+            return carry
+
+        low = min(lag for _, lag in table) if low is None else low
+        high = count + max(lag for _, lag in table) if high is None else high
+        lax.fori_loop(low, high, step, 0)
+
     def sent_wait(way, planes):
         pltpu.make_async_remote_copy(
             src_ref=tall.at[0:planes],
@@ -164,11 +176,6 @@
 
     @pl.when(is_end)
     def _():
-        for copy in own_norms:
-            copy.wait()
-        for copy in norm_copies(out, me):
-            copy.start()
-
         def raw_copy(c, s):
             return pltpu.make_async_remote_copy(
                 src_ref=spot(tall, c, s),
@@ -184,31 +191,32 @@
             finish(c, own(c, me) + decode(recv_v[back, c, me], n - 1), me)
             share_copy(out, c, me).start()
 
-        def end_step(j, carry):
-            for s in range(n - 1, 0, -1):
-
-                @pl.when(jnp.logical_and(j >= DEPTH, j < count + DEPTH))
+        def raw(s):
+            def act(c):
+                @pl.when(c >= DEPTH)
                 def _():
-                    raw_copy(j - DEPTH, seg(s)).wait_send()
-
-                @pl.when(j < count)
-                def _():
-                    raw_copy(j, seg(s)).start()
-
-            @pl.when(jnp.logical_and(j >= END_CLOSE, j < count + END_CLOSE))
-            def _():
-                close(j - END_CLOSE)
-
-            return carry
-
-        for t in range(T):
-            for copy in loads[t]:
-                copy.wait()
-            if t == 1:
-                for copy in held:
-                    copy.wait()
-            lax.fori_loop(t * halves, (t + 1) * halves, end_step, 0)
-        lax.fori_loop(count, count + max(DEPTH, END_CLOSE), end_step, 0)
+                    raw_copy(c - DEPTH, seg(s)).wait_send()
+
+                raw_copy(c, seg(s)).start()
+
+            return act
+
+        acts = {"raw3": raw(3), "raw2": raw(2), "raw1": raw(1), "close": close}
+        for copy in loads[0]:
+            copy.wait()
+        first = min(lag for _, lag in ENDS)
+        run(ENDS, acts, first, first + 1)
+        for copy in own_norms:
+            copy.wait()
+        for copy in norm_copies(out, me):
+            copy.start()
+        run(ENDS, acts, first + 1, first + halves)
+        for copy in sum(loads[1:], []) + held:
+            copy.wait()
+        run(ENDS, acts, first + halves)
+        for s in range(1, n):
+            for c in range(count - DEPTH, count):
+                raw_copy(c, seg(s)).wait_send()
         for copy in norm_copies(out, me):
             copy.wait_send()
         for s in range(1, n):
@@ -225,64 +233,58 @@
         for copy in sum(loads, []) + held:
             copy.wait()
 
-        def step(j, carry):
-            def at_lag(lag, act):
-                c = j - lag
-
-                @pl.when(jnp.logical_and(c >= 0, c < count))
-                def _():
-                    act(c)
-
-            def rs_out(c):
-                for i, s in enumerate((seg(3), seg(2))):
-                    sum_wait(out, c, s)
-                    total = own(c, s) + recv_v[out, c, s].astype(jnp.float32)
-                    send_v[i, c] = encode(total, 2)
-                    sum_copy(out, c, s, send_v.at[i, c]).start()
-
-            def rs_back(c):
-                s = seg(0)
-                sum_wait(back, c, s)
-                send_v[2, c] = encode(own(c, s) + decode(recv_v[back, c, s], 2), 3)
-                sum_copy(back, c, s, send_v.at[2, c]).start()
-
-            def close(c):
-                sum_wait(out, c, me)
-                total = own(c, me) + recv_v[out, c, me].astype(jnp.float32)
-                sum_wait(back, c, me)
-                finish(c, total + decode(recv_v[back, c, me], 2), me)
-                share_copy(out, c, me).start()
-                share_copy(back, c, me, True).start()
-
-            def pass_on(way, s, last):
-                def act(c):
-                    share_copy(way, c, s).wait_recv()
-                    share_copy(way, c, s, last).start()
-
-                return act
-
-            at_lag(RS_OUT, rs_out)
-            at_lag(RS_BACK, rs_back)
-            at_lag(FINISH, close)
-            at_lag(PASS_OUT, pass_on(out, seg(0), False))
-            at_lag(PASS_NEAR, pass_on(back, seg(2), True))
-            at_lag(PASS_FAR, pass_on(back, seg(3), True))
-            return carry
-
-        early = 2
-        lax.fori_loop(0, early, step, 0)
+        def sum_out(s):
+            def act(c):
+                sum_wait(out, c, seg(s))
+                total = own(c, seg(s)) + recv_v[out, c, seg(s)].astype(jnp.float32)
+                send_v[s - 2, c] = encode(total, 2)
+                sum_copy(out, c, seg(s), send_v.at[s - 2, c]).start()
+
+            return act
+
+        def sum_back(c):
+            s = seg(0)
+            sum_wait(back, c, s)
+            send_v[2, c] = encode(own(c, s) + decode(recv_v[back, c, s], 2), 3)
+            sum_copy(back, c, s, send_v.at[2, c]).start()
+
+        def close(c):
+            sum_wait(out, c, me)
+            total = own(c, me) + recv_v[out, c, me].astype(jnp.float32)
+            sum_wait(back, c, me)
+            finish(c, total + decode(recv_v[back, c, me], 2), me)
+            share_copy(out, c, me).start()
+            share_copy(back, c, me, True).start()
+
+        def pass_on(way, s, last):
+            def act(c):
+                share_copy(way, c, s).wait_recv()
+                share_copy(way, c, s, last).start()
+
+            return act
+
+        acts = {
+            "sum3": sum_out(3),
+            "sum2": sum_out(2),
+            "sum0": sum_back,
+            "close": close,
+            "pass0": pass_on(out, seg(0), False),
+            "pass2": pass_on(back, seg(2), True),
+            "pass3": pass_on(back, seg(3), True),
+        }
+        first = min(lag for _, lag in MIDDLES)
+        run(MIDDLES, acts, first, first + EARLY)
         for way, s in ((out, 0), (back, 2)):
             for copy in norm_copies(way, seg(s)):
                 copy.wait_recv()
             for copy in norm_copies(way, seg(s)):
                 copy.start()
-        lax.fori_loop(early, 2 * early, step, 0)
+        run(MIDDLES, acts, first + EARLY, first + 2 * EARLY)
         for copy in norm_copies(back, seg(3)):
             copy.wait_recv()
         for copy in norm_copies(back, seg(3)):
             copy.start()
-        last = max(RS_OUT, RS_BACK, FINISH, PASS_OUT, PASS_NEAR, PASS_FAR)
-        lax.fori_loop(2 * early, count + last, step, 0)
+        run(MIDDLES, acts, first + 2 * EARLY)
         for way, s in ((out, 0), (out, 1), (back, 1), (back, 2), (back, 3)):
             for copy in norm_copies(way, seg(s)):
                 copy.wait_send()
@@ -321,9 +323,9 @@
 
 def write(n, *refs):
     T = MATRICES
-    grown, step_v, state_v, stepped_norm_v, state_norm_v = refs[:5]
-    compute, stepped, state = refs[5 : 5 + T], refs[5 + T : 5 + 2 * T], refs[5 + 2 * T : 5 + 3 * T]
-    stepped_norm, state_norm, sems = refs[5 + 3 * T :]
+    grown, step_v, state_v, compute_norm_v, stepped_norm_v, state_norm_v = refs[:6]
+    compute, stepped, state = refs[6 : 6 + T], refs[6 + T : 6 + 2 * T], refs[6 + 2 * T : 6 + 3 * T]
+    compute_norm, stepped_norm, state_norm, flat, sems = refs[6 + 3 * T :]
     rows, cols = stepped[0].shape
     pairs = [(grown.at[t], compute[t]) for t in range(T - 1)]
     pairs += [
@@ -332,10 +334,12 @@
     ]
     pairs += [(step_v.at[t], stepped[t]) for t in range(T)]
     pairs += [(state_v.at[t], state[t]) for t in range(T)]
-    pairs += [(stepped_norm_v, stepped_norm), (state_norm_v, state_norm)]
+    pairs += [(stepped_norm_v, stepped_norm), (state_norm_v, state_norm), (flat, compute_norm)]
     copies = [pltpu.make_async_copy(*pair, sems.at[i]) for i, pair in enumerate(pairs)]
-    for copy in copies:
+    for copy in copies[:-1]:
         copy.start()
+    flat[...] = compute_norm_v[...].reshape(flat.shape).astype(flat.dtype)
+    copies[-1].start()
     for copy in copies:
         copy.wait()
 
@@ -399,16 +403,16 @@
         functools.partial(write, n),
         out_shape=[jax.ShapeDtypeStruct(p.shape, bf16) for p in partials]
         + [share] * (2 * T)
+        + [jax.ShapeDtypeStruct((whole,), bf16)]
         + [jax.ShapeDtypeStruct((1, cols), f32)] * 2,
-        in_specs=[inside] * 5,
-        out_specs=[anywhere] * (3 * T + 2),
-        scratch_shapes=[dma((3 * T + n + 1,))],
+        in_specs=[inside] * 6,
+        out_specs=[anywhere] * (3 * T + 3),
+        scratch_shapes=[pltpu.VMEM((whole,), bf16), dma((3 * T + n + 2,))],
         compiler_params=pltpu.CompilerParams(vmem_limit_bytes=1024 * 1024),
         name="write_out",
-    )(*kept[:3], *kept[4:])
+    )(*kept)
     compute, stepped, state = out[:T], out[T : 2 * T], out[2 * T : 3 * T]
-    stepped_norm, state_norm = out[3 * T :]
-    compute_norm = kept[3][0].astype(bf16)
+    compute_norm, stepped_norm, state_norm = out[3 * T :]
     return (*compute, compute_norm, *stepped, stepped_norm[0], *state, state_norm[0])
 
 

time: 70.4 us -> 64.2 us (0.912)
  Pallas kernels: 69 us -> 63.4 us
    pallas_call x1, Pallas kernels: 66.9 us -> 61.2 us  [line(): pl.pallas_call(functools.partial(kernel, n, halves), out_shape=[pltpu.VME...]
where the time goes in v2:
time: 64.2 us; the launch traced here: 64 us
  Pallas kernels  63.4 us (99%)
  between operations  0.66 us (1%)
    pallas_call x1, Pallas kernels, line(): pl.pallas_call(functools.partial(kernel, n, halves), out_shape=[pltpu.VME...  61.2 us
    pallas_call x1, Pallas kernels, line(): pl.pallas_call(functools.partial(write, n), out_shape=[jax.ShapeDtypeStru...  2.17 us

profile of v2, /device:TPU:0, one launch (start us, length us, event | category | flops | bytes accessed | tf_op | source)
XLA Modules:
  0.0 64.0 jit_solution(12723235229694557767)
XLA Ops:
  0.7 61.2 %line_step.1 = (bf16[4,1024,256]{2,1,0:T(8,128)(2,1)S(1)}, f32[4,256,256]{2,1,0:T(8,128)S(1)}, f32[4,256,256]{2,1,0:T(8,128)S(1)}, f32[1,1024]{1,0:T(1,128)S(1)}...) custom-call(bf16[1024,256]{1,0:T(8,128)(2,1)} %bitcast.8, bf16[1024,256]{1,0:T(8,128)(2,1)} %bitcast.9, ...), custom_call_target="tpu_custom_call" | custom-call | tf_op jit(solution)/shard_map/line_step/pallas_call | solution.py:357
  61.9 2.2 %write_out.1 = (bf16[1024,256]{1,0:T(8,128)(2,1)}, bf16[1024,256]{1,0:T(8,128)(2,1)}, bf16[1024,256]{1,0:T(8,128)(2,1)}, bf16[256,1024]{1,0:T(8,128)(2,1)}, f32[...) custom-call(bf16[4,1024,256]{2,1,0:T(8,128)(2,1)S(1)} %get-tuple-ele, ...), custom_call_target="tpu_custom_call" | custom-call | tf_op jit(solution)/shard_map/write_out/pallas_call | solution.py:402

commit v3 on v2

--- a/solution.py
+++ b/solution.py
@@ -12,8 +12,8 @@
 HALVES = 4
 DEPTH = 2
 EARLY = 3
-ENDS = (("raw3", 0), ("close", 47), ("raw1", 3), ("raw2", 0))
-MIDDLES = (("pass2", 7), ("close", 4), ("pass3", 26), ("pass0", 18), ("sum3", 0), ("sum0", 2), ("sum2", 1))
+ENDS = (("raw2", 0), ("raw1", 2), ("raw3", 0), ("close", 76))
+MIDDLES = (("close", 3), ("pass0", 18), ("pass2", 5), ("sum3", 1), ("sum0", 3), ("sum2", 0), ("pass3", 24))
 MESH = pl.DeviceIdType.MESH
 LINK = jnp.bfloat16
 MATRICES = 4

time: 64.2 us -> 63.3 us (0.986)
  Pallas kernels: 63.4 us -> 62.5 us
    pallas_call x1, Pallas kernels: 61.2 us -> 60.3 us  [line(): pl.pallas_call(functools.partial(kernel, n, halves), out_shape=[pltpu.VME...]
where the time goes in v3:
time: 63.3 us; the launch traced here: 63.2 us
  Pallas kernels  62.5 us (99%)
  between operations  0.66 us (1%)
    pallas_call x1, Pallas kernels, line(): pl.pallas_call(functools.partial(kernel, n, halves), out_shape=[pltpu.VME...  60.3 us
    pallas_call x1, Pallas kernels, line(): pl.pallas_call(functools.partial(write, n), out_shape=[jax.ShapeDtypeStru...  2.17 us

profile of v3, /device:TPU:0, one launch (start us, length us, event | category | flops | bytes accessed | tf_op | source)
XLA Modules:
  0.0 63.2 jit_solution(6637905590353184942)
XLA Ops:
  0.7 60.3 %line_step.1 = (bf16[4,1024,256]{2,1,0:T(8,128)(2,1)S(1)}, f32[4,256,256]{2,1,0:T(8,128)S(1)}, f32[4,256,256]{2,1,0:T(8,128)S(1)}, f32[1,1024]{1,0:T(1,128)S(1)}...) custom-call(bf16[1024,256]{1,0:T(8,128)(2,1)} %bitcast.8, bf16[1024,256]{1,0:T(8,128)(2,1)} %bitcast.9, ...), custom_call_target="tpu_custom_call" | custom-call | tf_op jit(solution)/shard_map/line_step/pallas_call | solution.py:357
  61.0 2.2 %write_out.1 = (bf16[1024,256]{1,0:T(8,128)(2,1)}, bf16[1024,256]{1,0:T(8,128)(2,1)}, bf16[1024,256]{1,0:T(8,128)(2,1)}, bf16[256,1024]{1,0:T(8,128)(2,1)}, f32[...) custom-call(bf16[4,1024,256]{2,1,0:T(8,128)(2,1)S(1)} %get-tuple-ele, ...), custom_call_target="tpu_custom_call" | custom-call | tf_op jit(solution)/shard_map/write_out/pallas_call | solution.py:402

commit v4 on v3

--- a/solution.py
+++ b/solution.py
@@ -27,12 +27,15 @@
 
 
 def encode(value, terms):
-    gain = TOP / (terms * LIMIT)
-    return jnp.exp2(value * gain).astype(LINK)
+    gain = 2 * TOP / (terms * LIMIT)
+    size = jnp.exp2(jnp.abs(value) * gain - TOP)
+    return jnp.where(value < 0, -size, size).astype(LINK)
 
 
 def decode(code, terms):
-    return jnp.log2(code.astype(jnp.float32)) * (terms * LIMIT / TOP)
+    code = code.astype(jnp.float32)
+    size = (jnp.log2(jnp.abs(code)) + TOP) * (terms * LIMIT / (2 * TOP))
+    return jnp.where(code < 0, -size, size)
 
 
 def kernel(n, halves, *refs):

time: 63.3 us -> 63.3 us (level)
  no operation moved by 1% of the time
where the time goes in v4:
time: 63.3 us; the launch traced here: 63.2 us
  Pallas kernels  62.5 us (99%)
  between operations  0.66 us (1%)
    pallas_call x1, Pallas kernels, line(): pl.pallas_call(functools.partial(kernel, n, halves), out_shape=[pltpu.VME...  60.3 us
    pallas_call x1, Pallas kernels, line(): pl.pallas_call(functools.partial(write, n), out_shape=[jax.ShapeDtypeStru...  2.17 us

profile of v4, /device:TPU:0, one launch (start us, length us, event | category | flops | bytes accessed | tf_op | source)
XLA Modules:
  0.0 63.2 jit_solution(1710128089865460850)
XLA Ops:
  0.7 60.3 %line_step.1 = (bf16[4,1024,256]{2,1,0:T(8,128)(2,1)S(1)}, f32[4,256,256]{2,1,0:T(8,128)S(1)}, f32[4,256,256]{2,1,0:T(8,128)S(1)}, f32[1,1024]{1,0:T(1,128)S(1)}...) custom-call(bf16[1024,256]{1,0:T(8,128)(2,1)} %bitcast.8, bf16[1024,256]{1,0:T(8,128)(2,1)} %bitcast.9, ...), custom_call_target="tpu_custom_call" | custom-call | tf_op jit(solution)/shard_map/line_step/pallas_call | solution.py:360
  61.0 2.2 %write_out.1 = (bf16[1024,256]{1,0:T(8,128)(2,1)}, bf16[1024,256]{1,0:T(8,128)(2,1)}, bf16[1024,256]{1,0:T(8,128)(2,1)}, bf16[256,1024]{1,0:T(8,128)(2,1)}, f32[...) custom-call(bf16[4,1024,256]{2,1,0:T(8,128)(2,1)S(1)} %get-tuple-ele, ...), custom_call_target="tpu_custom_call" | custom-call | tf_op jit(solution)/shard_map/write_out/pallas_call | solution.py:405
